TPU v7x, 32 devices: a whole 2x2x4 slice. The times are simulated.
32 devices in a mesh: obs: 8 (over z, x), bel: 4 (over y, core).
Axes of the slice: x: 2, y: 2, z: 4, core: 2. Of those that a mesh axis runs over, the one named last changes fastest.
Arguments:
- alpha_set: bfloat16 [2048, 2048], P('bel'), may hold values from -600 to 600
- transitions: bfloat16 [16, 2048, 2048], P(None, 'obs'), may hold values from 0.0009994507 to 1
- obs_weights: float32 [256, 16, 2048], P('obs'), may hold values from 0.01 to 1
- rewards: float32 [16, 2048], replicated, may hold values from -1 to 1
- chosen_idx: int32 [1536, 16, 256], P('bel', None, 'obs'), may hold values from 0 to 2047
- chosen_action: int32 [1536], P('bel'), may hold values from 0 to 15
Outputs:
- new_alpha: float32 [1536, 2048], P(('bel', 'obs'))
Inputs may be any that keep to these rules, and one draw needn't show every extreme that they name: `chosen_idx`: an index into the 2048 alpha vectors. `chosen_action`: an index into the 16 actions.
All inputs are finite; a program needn't handle non-finite values.
Results may differ from a plain program's by a relative error of at most 0.0003.
Values may be sent and summed in bfloat16 or wider, within the bound.
No kernel may reach another device: no remote copies, remote signals or barrier semaphores. Data moves between devices by JAX's collectives and lax.ppermute only.
A program may use at most 192 MiB of HBM per device.

v0:
```python
import jax
import jax.numpy as jnp
from jax import lax
from jax.sharding import PartitionSpec as P

discount = 0.95


def action_table(actions, count):
    return (actions[:, None] == jnp.arange(count, dtype=jnp.int32)[None, :]).astype(jnp.float32)


def picked_rows(indices, hot):
    chosen = jnp.sum(jnp.where(hot[:, :, None] > 0, indices, 0), axis=1)
    return chosen.T


def body(alpha_set, transitions, obs_weights, rewards, chosen_idx, chosen_action):
    actions = rewards.shape[0]
    states = rewards.shape[1]
    obs_local = obs_weights.shape[0]
    bel_rows = chosen_action.shape[0]
    trans_raw = transitions.astype(jnp.float32)
    action_hot = action_table(chosen_action, actions)
    picks = picked_rows(chosen_idx, action_hot).reshape(-1)
    piece = lax.all_gather(alpha_set, "bel", axis=0, tiled=True)
    count = piece.shape[0]
    onehot = (picks[:, None] == jnp.arange(count, dtype=jnp.int32)[None, :]).astype(jnp.bfloat16)
    chosen = jnp.dot(onehot, piece, preferred_element_type=jnp.float32)
    chosen = chosen.reshape(obs_local, bel_rows, states)
    obs_totals, trans_totals = lax.psum(
        (jnp.sum(obs_weights, axis=0), jnp.sum(trans_raw, axis=1)), "obs"
    )
    obs_prob = obs_weights / obs_totals[None, :, :]
    belief_prob = jnp.einsum("ba,oas->obs", action_hot, obs_prob, precision=lax.Precision.HIGHEST)
    partial_value = jnp.sum(belief_prob * chosen, axis=0)
    slice_w = lax.psum_scatter(partial_value, "obs", scatter_dimension=1, tiled=True)
    trans_prob = trans_raw / trans_totals[:, None, :]
    width = slice_w.shape[1]
    spread = (action_hot[:, :, None] * slice_w[:, None, :]).reshape(bel_rows, actions * width)
    table = trans_prob.reshape(actions * width, states)
    owned = bel_rows // lax.axis_size("obs")
    future = lax.psum_scatter(
        jnp.dot(spread, table, precision=lax.Precision.HIGHEST, preferred_element_type=jnp.float32),
        "obs",
        scatter_dimension=0,
        tiled=True,
    )
    own_hot = lax.dynamic_slice_in_dim(action_hot, lax.axis_index("obs") * owned, owned, 0)
    reward_rows = jnp.dot(
        own_hot, rewards, precision=lax.Precision.HIGHEST, preferred_element_type=jnp.float32
    )
    return reward_rows + discount * future


def solution(mesh):
    placed = (
        P("bel", None),
        P(None, "obs", None),
        P("obs", None, None),
        P(),
        P("bel", None, "obs"),
        P("bel"),
    )
    return jax.shard_map(
        body, mesh=mesh, in_specs=placed, out_specs=P(("bel", "obs"), None), check_vma=False
    )
```

profile of v0, /device:TPU:0, one launch (start us, length us, event | category | flops | bytes accessed | tf_op | source)
XLA Modules:
  0.0 457.6 jit_solution(5669605454711230280)
XLA Ops:
  7.4 0.0 copy-start
  7.4 0.0 all-gather.2.cloned.1.call-start
  7.4 0.7 all-gather.2.cloned.1.call-update
  8.1 0.0 all-reduce.3.cloned.1.call-start
  8.1 3.0 reduce_sum.36
  11.2 0.0 copy-start.3
  11.2 0.0 copy-start.1
  11.2 7.7 %convert_reduce_fusion = f32[16,2048]{1,0:T(8,128)} fusion(bf16[16,256,2048]{2,1,0:T(8,128)(2,1)} %param.7), kind=kLoop, calls=%fused_computation.6 | loop fusion | flops 16744448 | bytes 16908288 | tf_op jit(solution)/shard_map/reduce_sum | solution.py:32
  18.9 0.0 all-reduce.3.cloned.1.call-update
  18.9 0.0 reduce-scatter.3.cloned.1.call-start
  19.0 0.0 copy-done.3
  19.0 0.6 iota_compare_fusion.2
  19.6 0.0 copy-done.1
  19.6 0.1 select_reduce_fusion
  19.7 51.1 %all-gather.2.cloned.1.call-done = bf16[2048,2048]{1,0:T(8,128)(2,1)} async-done(((bf16[512,2048]{1,0:T(8,128)(2,1)}), bf16[2048,2048]{1,0:T(8,128)(2,1)}) %all-gather.2.cloned.1.call-update) | async-done | bytes 8388624 | tf_op jit(solution)/shard_map/all_gather | solution.py:26
  70.7 0.0 copy-start.4
  70.8 116.2 %fusion.1 = f32[12288,2048]{1,0:T(8,128)} fusion(bf16[2048,2048]{1,0:T(8,128)(2,1)} %all-gather.2.cloned.1.call-done, s32[12288]{0:T(1024)S(1)} %eq.38), kind=kOutput, calls=%fused_computation.3 | convolution fusion | flops 103104380928 | bytes 109101056 | tf_op jit(solution)/shard_map/dot_general | solution.py:29
  187.0 0.0 all-reduce.3.cloned.1.call-done
  187.0 0.0 copy-done.4
  187.0 0.0 copy-start.2
  187.0 62.6 %fusion = f32[384,2048]{1,0:T(8,128)} fusion(f32[32,384,2048]{2,1,0:T(8,128)} %bitcast.3, f32[32,16,2048]{2,1,0:T(8,128)} %param.8, f32[16,2048]{1,0:T(8,128)} %get-tuple-element.6, s32[384]{0:T(512)S(1)} %copy-done.4), kind=kOutput, calls=%fused_computation.1 | convolution fusion | flops 4882438144 | bytes 108135936 | tf_op jit(solution)/shard_map/ba,oas->obs/dot_general | solution.py:35
  249.6 0.0 copy-start.5
  249.6 0.0 reduce-scatter.3.cloned.1.call-update
  249.6 0.0 reduce-scatter.5.cloned.1.call-start
  249.6 75.1 %reduce-scatter.3.cloned.1.call-done = f32[384,256]{1,0:T(8,128)} async-done(((f32[384,2048]{1,0:T(8,128)}), f32[384,256]{1,0:T(8,128)}) %reduce-scatter.3.cloned.1.call-update) | async-done | bytes 393232 | tf_op jit(solution)/shard_map/reduce_scatter | solution.py:37
  324.8 0.0 copy-done.2
  324.8 1.9 fusion.30
  326.6 0.0 copy-done.5
  326.6 47.3 %fusion.9 = f32[384,2048]{1,0:T(8,128)} fusion(bf16[16,256,2048]{2,1,0:T(8,128)(2,1)} %param.7, f32[16,2048]{1,0:T(8,128)S(1)} %copy-done.5, f32[384,16,256]{2,0,1:T(8,128)S(1)} %fusion.30), kind=kOutput, calls=%fused_computation.13 | convolution fusion | flops 38671482880 | bytes 26345472 | tf_op jit(solution)/shard_map/dot_general | solution.py:44
  373.9 0.0 reduce-scatter.5.cloned.1.call-update
  374.0 73.8 %reduce-scatter.5.cloned.1.call-done = f32[48,2048]{1,0:T(8,128)} async-done(((f32[384,2048]{1,0:T(8,128)}), f32[48,2048]{1,0:T(8,128)}) %reduce-scatter.5.cloned.1.call-update) | async-done | bytes 393232 | tf_op jit(solution)/shard_map/reduce_scatter | solution.py:43
  447.8 0.0 copy-done
  447.8 2.2 convolution_add_fusion
  (1 shorter events, 0.0 us)
Async XLA Ops:
  7.4 440.4 %copy-start = (f32[16,2048]{1,0:T(8,128)S(1)}, f32[16,2048]{1,0:T(8,128)}, u32[]{:S(2)}) copy-start(f32[16,2048]{1,0:T(8,128)} %param.9) | copy-start | bytes 393220
  7.4 63.4 %all-gather.2.cloned.1.call-start = ((), (), s32[]{:S(2)}) async-start(), calls=%async_computation.2 | async-start | bytes 10485760 | tf_op jit(solution)/shard_map/all_gather | solution.py:26
  8.1 178.9 %all-reduce.3.cloned.1.call-start = ((), (), s32[]{:S(2)}) async-start(), calls=%async_computation.5 | async-start | bytes 524288 | tf_op jit(solution)/shard_map/psum | solution.py:31
  11.2 7.8 %copy-start.3 = (s32[384]{0:T(512)S(1)}, s32[384]{0:T(512)}, u32[]{:S(2)}) copy-start(s32[384]{0:T(512)} %param.11) | copy-start | bytes 4612
  11.2 8.4 %copy-start.1 = (s32[384,16,32]{0,2,1:T(8,128)S(1)}, s32[384,16,32]{0,2,1:T(8,128)}, u32[]{:S(2)}) copy-start(s32[384,16,32]{0,2,1:T(8,128)} %param.10) | copy-start | bytes 2359300
  18.9 305.8 %reduce-scatter.3.cloned.1.call-start = ((), (), s32[]{:S(2)}) async-start(), calls=%async_computation.3 | async-start | bytes 3538944 | tf_op jit(solution)/shard_map/reduce_scatter | solution.py:37
  70.7 116.2 %copy-start.4 = (s32[384]{0:T(512)S(1)}, s32[384]{0:T(512)}, u32[]{:S(2)}) copy-start(s32[384]{0:T(512)} %param.11) | copy-start | bytes 4612
  187.0 137.8 %copy-start.2 = (f32[384,16]{0,1:T(8,128)S(1)}, f32[384,16]{0,1:T(8,128)}, u32[]{:S(2)}) copy-start(f32[384,16]{0,1:T(8,128)} %get-tuple-element.9) | copy-start | bytes 73732
  249.6 77.1 %copy-start.5 = (f32[16,2048]{1,0:T(8,128)S(1)}, f32[16,2048]{1,0:T(8,128)}, u32[]{:S(2)}) copy-start(f32[16,2048]{1,0:T(8,128)} %get-tuple-element.5) | copy-start | bytes 393220
  249.6 198.2 %reduce-scatter.5.cloned.1.call-start = ((), (), s32[]{:S(2)}) async-start(), calls=%async_computation.4 | async-start | bytes 3538944 | tf_op jit(solution)/shard_map/reduce_scatter | solution.py:43
Sparse Core Ops, SparseCore 0:
  9.7 60.9 all-gather.1
Sparse Core Ops, SparseCore 1:
  19.0 74.0 all-reduce.2
  249.7 75.0 reduce-scatter.2
  374.1 73.7 reduce-scatter.4
where the time goes:
time: 458 us
  matrix products  228 us (50%)
  waiting for transfers between devices  201 us (44%)
  between operations  15.1 us (3%)
  other arithmetic  13.3 us (3%)
    dot_general x1, matrix products, body(): chosen = jnp.dot(onehot, piece, preferred_element_type=jnp.float32)  116 us
    reduce_scatter x1, waiting for transfers between devices, body(): lax.psum_scatter(partial_value, 'obs', scatter_dimension=1, tiled=True)  75.1 us
    reduce_scatter x1, waiting for transfers between devices, body(): lax.psum_scatter(jnp.dot(spread, table, precision=lax.Precision.HIGHEST,...  73.8 us
    dot_general x1, matrix products, body(): jnp.einsum('ba,oas->obs', action_hot, obs_prob, precision=lax.Precision.H...  62.6 us
    all_gather x1, waiting for transfers between devices, body(): piece = lax.all_gather(alpha_set, 'bel', axis=0, tiled=True)  51.1 us
    dot_general x1, matrix products, body(): jnp.dot(spread, table, precision=lax.Precision.HIGHEST, preferred_element...  47.3 us
  transfers between devices with their start and end apart: 4, of which 3 were waited for; matrix products, arithmetic and copies ran while one was open for 28% of the time, Pallas kernels for 0%

commit v1 on v0

v1 whole, which is shorter than its diff:
```python
import functools
import math

import jax
import jax.numpy as jnp
from jax import lax
from jax.experimental import pallas as pl
from jax.experimental.pallas import tpu as pltpu
from jax.sharding import PartitionSpec as P

discount = 0.95
LANES = 128
WEIGHT_LOW = 0.01
SPAN = -math.log2(WEIGHT_LOW)
FULL = 32767.0
FINE = 8.0
DIRECT = 4


def log_code(values, top):
    place = (jnp.log2(values) - math.log2(top) + SPAN) * (65535.0 / SPAN)
    return (jnp.clip(jnp.round(place), 0.0, 65535.0) - 32768.0).astype(jnp.int32).astype(jnp.int16)


def log_value(code, top):
    place = code.astype(jnp.int32).astype(jnp.float32) + 32768.0
    return jnp.exp2(place * (SPAN / 65535.0) + (math.log2(top) - SPAN))


def step_code(values, axis):
    most = jnp.max(jnp.abs(values), axis=axis, keepdims=True)
    power = jnp.ceil(jnp.log2(jnp.maximum(most, 1e-30)) * FINE + 0.01)
    steps = jnp.round(values * (jnp.exp2(power * (-1.0 / FINE)) * FULL))
    steps = jnp.clip(steps, -FULL, FULL)
    return power, steps.astype(jnp.int32).astype(jnp.int16)


def step_value(code, power):
    scale = jnp.exp2(power.astype(jnp.int32).astype(jnp.float32) * (1.0 / FINE)) * (1.0 / FULL)
    return code.astype(jnp.int32).astype(jnp.float32) * scale


def to_short(power):
    return power.astype(jnp.int32).astype(jnp.int16)


def lane_code(values):
    power, code = step_code(values, -1)
    tail = jnp.broadcast_to(to_short(power), values.shape[:-1] + (LANES,))
    return jnp.concatenate([code, tail], axis=-1)


def lane_value(message, width):
    return step_value(message[..., :width], message[..., width : width + 1])


def columns_of(array, inner_at, inner, outer):
    width = array.shape[-1] // (inner * outer)
    cuts = [
        lax.dynamic_slice_in_dim(array, (place * inner + inner_at) * width, width, array.ndim - 1)
        for place in range(outer)
    ]
    return jnp.concatenate(cuts, axis=-1)


def selecting_kernel(depth, act_ref, idx_ref, kept_ref, got_ref, *refs):
    *pieces, out_ref, totals_ref, table, w_table, inverse = refs
    rows, half = out_ref.shape[0], out_ref.shape[1] * out_ref.shape[2]
    tile = out_ref.shape[1]
    actions = totals_ref.shape[0]
    kept_rows = kept_ref.shape[0]

    @pl.when(pl.program_id(0) == 0)
    def _():
        base = 0
        for piece in pieces:
            step = math.gcd(piece.shape[0], 32)

            def widen(at, carry, piece=piece, base=base, step=step):
                block = piece[pl.ds(at * step, step)].astype(jnp.float32)
                table[pl.ds((base + at * step) * tile, step * tile)] = block.reshape(step * tile, LANES)
                return carry

            lax.fori_loop(0, piece.shape[0] // step, widen, 0)
            base += piece.shape[0]

        def lay(at, block):
            block = block.reshape(actions, tile, LANES)
            for kind in range(actions):
                w_table[pl.ds((kind * depth + at) * tile, tile)] = block[kind]

        def keep(at, total):
            block = kept_ref[pl.ds(at * actions, actions)]
            lay(at, block)
            return total + block

        def take(at, total):
            block = log_value(got_ref[pl.ds(at * actions, actions)], 1.0)
            lay(at + kept_rows // actions, block)
            return total + block

        total = jnp.zeros((actions, half), jnp.float32)
        total = lax.fori_loop(0, kept_rows // actions, keep, total)
        total = lax.fori_loop(0, kept_rows // actions, take, total)
        totals_ref[...] = total
        inverse[...] = (1.0 / total).reshape(actions * tile, LANES)

    first = pl.program_id(0) * rows

    def one(row, carry):
        kind = act_ref[first + row]
        at = pl.multiple_of(kind * (depth * tile), depth * tile)
        listed = idx_ref.at[pl.ds((first + row) * depth, depth)]
        parts = []
        for o in range(depth):
            place = pl.multiple_of(listed[o], tile)
            term = w_table[pl.ds(at + o * tile, tile)] * table[pl.ds(place, tile)]
            if o < 4:
                parts.append(term)
            else:
                parts[o % 4] = parts[o % 4] + term
        total = parts[0]
        for part in parts[1:]:
            total = total + part
        out_ref[row] = total * inverse[pl.ds(pl.multiple_of(kind * tile, tile), tile)]
        return carry

    lax.fori_loop(0, rows, one, 0, unroll=4)


def select_and_sum(actions, picks, kept, got, pieces, count, kinds):
    half = kept.shape[1]
    depth = picks.shape[0] // count
    tiles = pieces[0].shape[1:]
    step = math.gcd(count, 32)
    known = sum(piece.shape[0] for piece in pieces)
    whole = [pl.BlockSpec(memory_space=pltpu.VMEM) for _ in range(2 + len(pieces))]
    return pl.pallas_call(
        functools.partial(selecting_kernel, depth),
        grid=(count // step,),
        in_specs=[
            pl.BlockSpec(memory_space=pltpu.SMEM),
            pl.BlockSpec(memory_space=pltpu.SMEM),
            *whole,
        ],
        out_specs=[
            pl.BlockSpec((step,) + tiles, lambda g: (g, 0, 0)),
            pl.BlockSpec((kinds, half), lambda g: (0, 0)),
        ],
        out_shape=[
            jax.ShapeDtypeStruct((count,) + tiles, jnp.float32),
            jax.ShapeDtypeStruct((kinds, half), jnp.float32),
        ],
        scratch_shapes=[
            pltpu.VMEM((known * tiles[0], LANES), jnp.float32),
            pltpu.VMEM((depth * kinds * tiles[0], LANES), jnp.float32),
            pltpu.VMEM((kinds * tiles[0], LANES), jnp.float32),
        ],
        compiler_params=pltpu.CompilerParams(
            dimension_semantics=("arbitrary",), vmem_limit_bytes=48 * 1024 * 1024
        ),
        name="select_and_sum",
    )(actions, picks, kept, got, *pieces)


def body(alpha_set, transitions, obs_weights, rewards, chosen_idx, chosen_action):
    actions, states = rewards.shape
    obs_local = obs_weights.shape[0]
    bel_rows = chosen_action.shape[0]
    known_local = alpha_set.shape[0]
    ranks = lax.axis_size("obs")
    groups = lax.axis_size("bel")
    inner = 2
    outer = ranks // inner
    me = lax.axis_index("obs")
    outer_at, inner_at = me // inner, lax.rem(me, inner)
    seat = lax.axis_index("bel")
    width = states // ranks
    half = states // inner
    tiles = (half // LANES, LANES)
    depth = obs_local * inner
    owned = bel_rows // ranks

    def swap_inner(array):
        return lax.ppermute(array, "obs", [(i, i ^ 1) for i in range(ranks)])

    def shift_outer(array, k):
        hops = [(i, ((i // inner + k) % outer) * inner + i % inner) for i in range(ranks)]
        return lax.ppermute(array, "obs", hops)

    def exchange_outer(blocks):
        if outer <= DIRECT:
            return [shift_outer(blocks(lax.rem(outer_at + k, outer)), k) for k in range(1, outer)]
        teams = [[q * inner + r for q in range(outer)] for r in range(inner)]
        sent = jnp.stack([blocks(jnp.int32(place)) for place in range(outer)])
        got = lax.all_to_all(sent, "obs", 0, 0, tiled=True, axis_index_groups=teams)
        got = lax.dynamic_slice_in_dim(jnp.concatenate([got, got]), outer_at, outer, 0)
        return [got[k] for k in range(1, outer)]

    mine = columns_of(alpha_set, inner_at, inner, outer).reshape((known_local,) + tiles)
    pieces, order, distance = [mine], [0], groups // 2
    while distance:
        hops = [(i, i ^ distance) for i in range(groups)]
        pieces = pieces + [lax.ppermute(piece, "bel", hops) for piece in pieces]
        order = order + [place ^ distance for place in order]
        distance //= 2

    action_hot = (chosen_action[:, None] == jnp.arange(actions, dtype=jnp.int32)[None, :])
    picks = jnp.sum(jnp.where(action_hot[:, :, None], chosen_idx, 0), axis=1)
    action_hot = action_hot.astype(jnp.float32)

    kept = columns_of(obs_weights, inner_at, inner, outer).reshape(obs_local * actions, half)
    given = log_code(columns_of(obs_weights, 1 - inner_at, inner, outer), 1.0)
    given = given.reshape(obs_local * actions, half)
    listed = picks.astype(jnp.int16).reshape(-1)
    pad = -listed.shape[0] % (16 * half)
    listed_rows = jnp.pad(listed, (0, pad)).reshape(-1, half)
    got = swap_inner(jnp.concatenate([given, listed_rows], axis=0))
    got_picks = got[obs_local * actions :].reshape(-1)[: listed.shape[0]].astype(jnp.int32).reshape(bel_rows, obs_local)

    share = jnp.sum(transitions.astype(jnp.float32), axis=1)
    if outer <= DIRECT:
        trans_totals = share
        for k in range(1, outer):
            trans_totals = trans_totals + shift_outer(share, k)
        trans_totals = trans_totals + swap_inner(trans_totals)
    else:
        trans_totals = lax.psum(share, "obs")

    both_picks = jnp.concatenate([picks, got_picks], axis=1)
    block, inside = both_picks // known_local, lax.rem(both_picks, known_local)
    relative = block ^ seat
    place = jnp.zeros_like(relative)
    for at, member in enumerate(order):
        place = jnp.where(relative == member, at, place)
    rows = (place * known_local + inside) * tiles[0]
    rows, trans_totals = lax.optimization_barrier((rows, trans_totals))
    shares, here_totals = select_and_sum(
        chosen_action, rows.reshape(-1), kept, got, pieces, bel_rows, actions
    )
    shares = shares.reshape(bel_rows, half)

    power, code = step_code(shares, 0)
    message = jnp.concatenate(
        [code, log_code(here_totals, float(depth)), jnp.broadcast_to(to_short(power), (16, half))], axis=0
    )
    received = exchange_outer(lambda q: lax.dynamic_slice_in_dim(message, q * width, width, 1))
    parts = [lax.dynamic_slice_in_dim(shares, outer_at * width, width, 1)]
    totals = [lax.dynamic_slice_in_dim(here_totals, outer_at * width, width, 1)]
    for block in received:
        parts.append(step_value(block[:bel_rows], block[bel_rows + actions : bel_rows + actions + 1]))
        totals.append(log_value(block[bel_rows : bel_rows + actions], float(depth)))
    factors = jnp.dot(action_hot, jnp.concatenate(totals, axis=1), precision=lax.Precision.HIGHEST)
    above, below = 0.0, 0.0
    for at, part in enumerate(parts):
        factor = factors[:, at * width : (at + 1) * width]
        above, below = above + factor * part, below + factor
    weighted = above / below

    upper = lax.reduce_precision(weighted, 8, 7)
    lower = weighted - upper
    halves = jnp.stack([upper, lower]).astype(jnp.bfloat16)
    spread = (action_hot.astype(jnp.bfloat16)[None, :, :, None] * halves[:, :, None, :]).reshape(
        2 * bel_rows, actions * width
    )
    moved = jnp.dot(
        spread, transitions.reshape(actions * width, states), preferred_element_type=jnp.float32
    )
    inverse = jnp.dot(action_hot, 1.0 / trans_totals, precision=lax.Precision.HIGHEST)
    future = (moved[:bel_rows] + moved[bel_rows:]) * inverse

    future = future.reshape(outer, inner, owned, states)
    ours = lax.dynamic_index_in_dim(future, inner_at, 1, keepdims=False)
    theirs = lane_code(lax.dynamic_index_in_dim(future, 1 - inner_at, 1, keepdims=False))
    ours = ours + lane_value(swap_inner(theirs), states)
    coded = lane_code(ours)
    total = lax.dynamic_index_in_dim(ours, outer_at, 0, keepdims=False)
    for block in exchange_outer(lambda q: lax.dynamic_index_in_dim(coded, q, 0, keepdims=False)):
        total = total + lane_value(block, states)
    own_hot = lax.dynamic_slice_in_dim(action_hot, me * owned, owned, 0)
    reward_rows = jnp.dot(own_hot, rewards, precision=lax.Precision.HIGHEST)
    return reward_rows + discount * total


def solution(mesh):
    placed = (
        P("bel", None),
        P(None, "obs", None),
        P("obs", None, None),
        P(),
        P("bel", None, "obs"),
        P("bel"),
    )
    return jax.shard_map(
        body, mesh=mesh, in_specs=placed, out_specs=P(("bel", "obs"), None), check_vma=False
    )
```

time: 458 us -> 172 us (0.38)
  matrix products: 228 us -> 21 us
  waiting for transfers between devices: 201 us -> 56.7 us
  Pallas kernels: 0 us -> 27.6 us
  starting transfers between devices: 0.13 us -> 19.3 us
  local copies, waits for them, and re-layouts: 0.03 us -> 18.8 us
  between operations: 15.1 us -> 0.37 us
  other arithmetic: 13.3 us -> 25.7 us
    dot_general x4, matrix products: 228 us -> 21 us  [the longest x1 16 us: body(): jnp.dot(spread, transitions.reshape(actions * width, states), preferred_e...]
    reduce_scatter x2 -> x0, waiting for transfers between devices: 149 us -> none  [the longest x1 75.1 us: body(): lax.psum_scatter(partial_value, 'obs', scatter_dimension=1, tiled=True)]
    ppermute x0 -> x15, waiting for transfers between devices: none -> 56.7 us  [the longest x9 36.4 us: shift_outer(): return lax.ppermute(array, 'obs', hops)]
    all_gather x1 -> x0, waiting for transfers between devices: 51.1 us -> none  [body(): piece = lax.all_gather(alpha_set, 'bel', axis=0, tiled=True)]
    pallas_call x0 -> x1, Pallas kernels: none -> 27.6 us  [select_and_sum(): pl.pallas_call(functools.partial(selecting_kernel, depth), grid=(count //...]
    ppermute x0 -> x15, starting transfers between devices: none -> 19.3 us  [the longest x9 13 us: shift_outer(): return lax.ppermute(array, 'obs', hops)]
    unnamed x12 -> x27, local copies, waits for them, and re-layouts: 0.02 us -> 8.42 us
    dynamic_slice x0 -> x4, local copies, waits for them, and re-layouts: none -> 6.25 us  [the longest x2 5.39 us: columns_of(): lax.dynamic_slice_in_dim(array, (place * inner + inner_at) * width, width...]
  transfers between devices with their start and end apart: 4 -> 15, of which waited for: 3 -> 10; matrix products, arithmetic and copies ran while one was open for 28% -> 14% of each run, Pallas kernels for 0% -> 0%
where the time goes in v1:
time: 172 us; the launch traced here: 169 us
  waiting for transfers between devices  56.7 us (33%)
  Pallas kernels  27.6 us (16%)
  other arithmetic  25.7 us (15%)
  matrix products  21 us (12%)
  starting transfers between devices  19.3 us (11%)
  local copies, waits for them, and re-layouts  18.8 us (11%)
    ppermute x9, waiting for transfers between devices, shift_outer(): return lax.ppermute(array, 'obs', hops)  36.4 us
    pallas_call x1, Pallas kernels, select_and_sum(): pl.pallas_call(functools.partial(selecting_kernel, depth), grid=(count //...  27.6 us
    ppermute x3, waiting for transfers between devices, swap_inner(): return lax.ppermute(array, 'obs', [(i, i ^ 1) for i in range(ranks)])  20.1 us
    dot_general x1, matrix products, body(): jnp.dot(spread, transitions.reshape(actions * width, states), preferred_e...  16 us
    ppermute x9, starting transfers between devices, shift_outer(): return lax.ppermute(array, 'obs', hops)  13 us
    unnamed x27, local copies, waits for them, and re-layouts  8.42 us
    reduce_sum x1, other arithmetic, body(): share = jnp.sum(transitions.astype(jnp.float32), axis=1)  6.98 us
    dynamic_slice x2, local copies, waits for them, and re-layouts, columns_of(): lax.dynamic_slice_in_dim(array, (place * inner + inner_at) * width, width...  5.39 us
  transfers between devices with their start and end apart: 15, of which 10 were waited for; matrix products, arithmetic and copies ran while one was open for 14% of the time, Pallas kernels for 0%

profile of v1, /device:TPU:0, one launch (start us, length us, event | category | flops | bytes accessed | tf_op | source)
XLA Modules:
  0.0 169.4 jit_solution(2812558819860583215)
XLA Ops:
  0.0 1.3 constant_dynamic-slice_fusion.7
  1.3 0.1 maximum_bitcast_fusion
  1.5 0.3 copy.42
  1.8 3.1 %collective-permute-start.5 = (bf16[512,8,128]{2,1,0:T(8,128)(2,1)S(1)}, bf16[512,8,128]{2,1,0:T(8,128)(2,1)S(1)}, u32[]{:S(2)}, u32[]{:S(2)}) collective-permute-start(bf16[512,8,128]{2,1,0:T(8,128)(2,1)S(1)} %bitcast.69), channel_id=1, source_target_pairs={{0,2},{1,3},{2,0},{3,1},{4,6},{5,7},{6,4},{7,5},{8,10},{9,11},{10,... | collective-permute-start | bytes 3145736 | tf_op jit(solution)/shard_map/ppermute | solution.py:204
  4.9 0.6 copy-done.6
  5.5 0.2 copy.31
  5.9 4.1 %constant_dynamic-slice_fusion.11 = (f32[32,16,256]{2,1,0:T(8,128)}, f32[32,16,256]{2,1,0:T(8,128)}, f32[32,16,256]{2,1,0:T(8,128)S(1)}, f32[32,16,256]{2,1,0:T(...) fusion(f32[32,16,2048]{2,1,0:T(8,128)} %param.8, ...), kind=kLoop, calls=%fused_computation.102 | loop fusion | bytes 8388640 | tf_op jit(solution)/shard_map/dynamic_slice | solution.py:60
  10.0 0.7 fusion.8
  10.7 1.1 pad_add_fusion
  11.8 1.5 collective-permute-start
  13.3 7.0 %convert_reduce_fusion = f32[16,2048]{1,0:T(8,128)S(1)} fusion(bf16[16,256,2048]{2,1,0:T(8,128)(2,1)} %param.7), kind=kLoop, calls=%fused_computation | loop fusion | flops 16744448 | bytes 16908288 | tf_op jit(solution)/shard_map/reduce_sum | solution.py:221
  20.3 3.7 %collective-permute-start.3 = (f32[16,2048]{1,0:T(8,128)S(1)}, f32[16,2048]{1,0:T(8,128)S(1)}, u32[]{:S(2)}, u32[]{:S(2)}) collective-permute-start(f32[16,2048]{1,0:T(8,128)S(1)} %convert_reduce_fusion), channel_id=1, source_target_pairs={{0,24},{4,28},{8,0},{12,4},{16,8},{20,12},{24,16},{28,20},{1,25},{... | collective-permute-start | bytes 393224 | tf_op jit(solution)/shard_map/ppermute | solution.py:189
  23.9 1.0 collective-permute-start.1
  24.9 2.9 %collective-permute-done.3 = f32[16,2048]{1,0:T(8,128)S(1)} collective-permute-done((f32[16,2048]{1,0:T(8,128)S(1)}, f32[16,2048]{1,0:T(8,128)S(1)}, u32[]{:S(2)}, u32[]{:S(2)}) %collective-permute-start.3) | collective-permute-done | bytes 131104 | tf_op jit(solution)/shard_map/ppermute | solution.py:189
  27.8 0.2 collective-permute-done.5.refs_1_
  28.0 0.5 copy-done.9
  28.5 6.4 %collective-permute-done.2 = f32[16,2048]{1,0:T(8,128)} collective-permute-done((f32[16,2048]{1,0:T(8,128)S(1)}, f32[16,2048]{1,0:T(8,128)}, u32[]{:S(2)}, u32[]{:S(2)}) %collective-permute-start.2) | collective-permute-done | bytes 131104 | tf_op jit(solution)/shard_map/ppermute | solution.py:189
  34.8 1.1 add_add_fusion
  35.9 0.6 collective-permute-start.4
  36.5 3.1 %pad_maximum_fusion = f32[32,16,1024]{2,1,0:T(8,128)} fusion(f32[32,16,256]{2,1,0:T(8,128)} %get-tuple-element.23, f32[32,16,256]{2,1,0:T(8,128)} %get-tuple-element.24, f32[32,16,256]{2,1,0:T(8,128)} %get-tuple-element.18, f32[32,16,256]{2,1,0:T(8,128)} %get-tuple-element.17), kind=kLoop, calls=%fused_computation.14 | loop fusion | flops 1572864 | bytes 4194304 | tf_op jit(solution)/shard_map/concatenate | solution.py:63
  39.6 1.3 collective-permute-done.4
  40.9 0.7 add.242
  41.6 0.6 slice_convert_fusion
  42.2 0.9 reshape.200
  43.2 0.7 copy.32
  43.9 0.9 add_multiply_fusion
  44.8 0.8 copy.33
  45.6 1.0 reshape.194.idx_ref
  46.7 27.6 %select_and_sum.1 = (f32[384,8,128]{2,1,0:T(8,128)}, f32[16,1024]{1,0:T(8,128)S(1)}) custom-call(s32[384]{0:T(512)S(1)} %copy-done.1, s32[24576]{0:T(1024)S(1)} %reshape.194.idx_ref, f32[512,1024]{1,0:T(8,128)} %bitcast.79, s16[528,1024]{1,0:T(8,128)(2,1)S(1)} %collective-permute-done.got_ref, bf16[512,8,128]{2,1,0:T(8,128)(2,1)S(1)} %bitcast.71, ...), custom_call_target="tpu_custom_call" | custom-call | tf_op jit(solution)/shard_map/select_and_sum/pallas_call | solution.py:138
  74.2 1.6 abs_reduce_fusion.1
  75.9 0.2 copy-done.2
  76.1 0.4 convert_convert_fusion.1
  76.6 0.9 constant_dynamic-slice_fusion.2
  77.5 0.8 collective-permute-start.8
  78.2 0.1 copy.30
  78.4 0.3 copy.52
  78.7 0.6 copy-done.8
  79.3 3.1 %collective-permute-start.10 = (s16[416,256]{1,0:T(8,128)(2,1)S(1)}, s16[416,256]{1,0:T(8,128)(2,1)S(1)}, u32[]{:S(2)}, u32[]{:S(2)}) collective-permute-start(s16[416,256]{1,0:T(8,128)(2,1)S(1)} %copy-done.8), channel_id=1, source_target_pairs={{0,24},{4,28},{8,0},{12,4},{16,8},{20,12},{24,16},{28,20},{1,25},{... | collective-permute-start | bytes 638984 | tf_op jit(solution)/shard_map/ppermute | solution.py:189
  82.4 0.7 collective-permute-start.9
  83.0 4.7 %collective-permute-done.8 = s16[416,256]{1,0:T(8,128)(2,1)} collective-permute-done((s16[416,256]{1,0:T(8,128)(2,1)}, s16[416,256]{1,0:T(8,128)(2,1)}, u32[]{:S(2)}, u32[]{:S(2)}) %collective-permute-start.8) | collective-permute-done | bytes 213024 | tf_op jit(solution)/shard_map/ppermute | solution.py:189
  87.7 0.7 multiply_exponential_fusion.2
  88.4 1.2 collective-permute-done.10
  89.6 9.1 %collective-permute-done.9 = s16[416,256]{1,0:T(8,128)(2,1)S(1)} collective-permute-done((s16[416,256]{1,0:T(8,128)(2,1)S(1)}, s16[416,256]{1,0:T(8,128)(2,1)S(1)}, u32[]{:S(2)}, u32[]{:S(2)}) %collective-permute-start.9) | collective-permute-done | bytes 213024 | tf_op jit(solution)/shard_map/ppermute | solution.py:189
  98.7 0.8 fusion.29
  99.6 0.7 fusion.54
  100.3 1.3 fusion.25
  101.7 1.1 broadcast_multiply_fusion
  102.8 4.5 %copy.44 = bf16[96,8,16,256]{3,1,2,0:T(8,128)(2,1)S(1)} copy(bf16[96,8,16,256]{3,2,1,0:T(8,128)(2,1)S(1)} %bitcast.72) | data formatting | bytes 12582912
  107.2 16.0 %fusion.57 = f32[768,2048]{1,0:T(8,128)S(1)} fusion(bf16[768,4096]{1,0:T(8,128)(2,1)S(1)} %bitcast.80, bf16[4096,2048]{1,0:T(8,128)(2,1)} %bitcast.76), kind=kOutput, calls=%fused_computation.134 | convolution fusion | flops 12884901888 | bytes 29360128 | tf_op jit(solution)/shard_map/dot_general | solution.py:266
  123.2 1.8 %fusion = f32[384,2048]{1,0:T(8,128)S(1)} fusion(f32[768,2048]{1,0:T(8,128)S(1)} %fusion.57, f32[16,2048]{1,0:T(8,128)S(1)} %copy-done.5, s32[384]{0:T(512)S(1)} %copy-done.1), kind=kOutput, calls=%fused_computation.2 | convolution fusion | flops 152606720 | bytes 9569792 | tf_op jit(solution)/shard_map/dot_general | solution.py:269
  125.0 0.2 fusion.9
  125.3 0.3 fusion.13
  125.6 1.0 pad_add_fusion.2
  126.6 1.1 collective-permute-start.11
  127.7 18.7 %collective-permute-done.11 = s16[4,48,2176]{2,1,0:T(8,128)(2,1)} collective-permute-done((s16[4,48,2176]{2,1,0:T(8,128)(2,1)}, s16[4,48,2176]{2,1,0:T(8,128)(2,1)}, u32[]{:S(2)}, u32[]{:S(2)}) %collective-permute-start.11) | collective-permute-done | bytes 835616 | tf_op jit(solution)/shard_map/ppermute | solution.py:185
  146.5 0.8 exponential_multiply_fusion
  147.4 1.7 abs_reduce_fusion
  149.1 1.2 copy-done.3
  150.2 0.2 convert_convert_fusion
  150.7 1.5 collective-permute-start.13
  152.2 2.3 %collective-permute-start.14 = (s16[48,2176]{1,0:T(8,128)(2,1)S(1)}, s16[48,2176]{1,0:T(8,128)(2,1)S(1)}, u32[]{:S(2)}, u32[]{:S(2)}) collective-permute-start(s16[48,2176]{1,0:T(8,128)(2,1)S(1)} %get-tuple-element.34), channel_id=1, source_target_pairs={{0,24},{4,28},{8,0},{12,4},{16,8},{20,12},{24,16},{28,20},{1,25},{... | collective-permute-start | bytes 626696 | tf_op jit(solution)/shard_map/ppermute | solution.py:189
  154.5 6.0 %collective-permute-done.12 = s16[48,2176]{1,0:T(8,128)(2,1)S(1)} collective-permute-done((s16[48,2176]{1,0:T(8,128)(2,1)S(1)}, s16[48,2176]{1,0:T(8,128)(2,1)S(1)}, u32[]{:S(2)}, u32[]{:S(2)}) %collective-permute-start.12) | collective-permute-done | bytes 208928 | tf_op jit(solution)/shard_map/ppermute | solution.py:189
  160.7 6.2 %collective-permute-done.13 = s16[48,2176]{1,0:T(8,128)(2,1)S(1)} collective-permute-done((s16[48,2176]{1,0:T(8,128)(2,1)S(1)}, s16[48,2176]{1,0:T(8,128)(2,1)S(1)}, u32[]{:S(2)}, u32[]{:S(2)}) %collective-permute-start.13) | collective-permute-done | bytes 208928 | tf_op jit(solution)/shard_map/ppermute | solution.py:189
  167.0 2.4 %convolution_add_fusion = f32[48,2048]{1,0:T(8,128)} fusion(f32[16,2048]{1,0:T(8,128)S(1)} %copy-done, f32[4,48,2048]{2,1,0:T(8,128)} %copy-done.3, s32[]{:T(128)S(6)} %select_n.111, s16[48,2176]{1,0:T(8,128)(2,1)S(1)} %collective-permute-done.14, s16[48,2176]{1,0:T(8,128)(2,1)S(1)} %collective-permute-done.13, ...), kind=kOutput, calls=%fused_computation.4 | convolution fusion | flops 20250624 | bytes 1510920 | tf_op jit(solution)/shard_map/dot_general | solution.py:281
  (53 shorter events, 1.2 us)
Async XLA Ops:
  0.0 167.0 %copy-start = (f32[16,2048]{1,0:T(8,128)S(1)}, f32[16,2048]{1,0:T(8,128)}, u32[]{:S(2)}) copy-start(f32[16,2048]{1,0:T(8,128)} %param.9) | copy-start | bytes 393220
  1.3 3.5 %copy-start.1 = (s32[384]{0:T(512)S(1)}, s32[384]{0:T(512)}, u32[]{:S(2)}) copy-start(s32[384]{0:T(512)} %act_ref.1) | copy-start | bytes 4612
  1.3 3.5 %copy-start.4 = (s32[384,16,32]{0,2,1:T(8,128)S(1)}, s32[384,16,32]{0,2,1:T(8,128)}, u32[]{:S(2)}) copy-start(s32[384,16,32]{0,2,1:T(8,128)} %param.10) | copy-start | bytes 2359300
  1.8 26.2 %collective-permute-start.5 = (bf16[512,8,128]{2,1,0:T(8,128)(2,1)S(1)}, bf16[512,8,128]{2,1,0:T(8,128)(2,1)S(1)}, u32[]{:S(2)}, u32[]{:S(2)}) collective-permute-start(bf16[512,8,128]{2,1,0:T(8,128)(2,1)S(1)} %bitcast.69), channel_id=1, source_target_pairs={{0,2},{1,3},{2,0},{3,1},{4,6},{5,7},{6,4},{7,5},{8,10},{9,11},{10,... | collective-permute-start | bytes 3145736 | tf_op jit(solution)/shard_map/ppermute | solution.py:204
  4.9 0.6 copy-start.6
  11.8 29.8 %collective-permute-start = (s16[528,1024]{1,0:T(8,128)(2,1)}, s16[528,1024]{1,0:T(8,128)(2,1)S(1)}, u32[]{:S(2)}, u32[]{:S(2)}) collective-permute-start(s16[528,1024]{1,0:T(8,128)(2,1)} %pad_add_fusion), channel_id=1, source_target_pairs={{0,4},{4,0},{8,12},{12,8},{16,20},{20,16},{24,28},{28,24},{1,5},{5... | collective-permute-start | bytes 3244040 | tf_op jit(solution)/shard_map/ppermute | solution.py:185
  20.3 7.5 %collective-permute-start.3 = (f32[16,2048]{1,0:T(8,128)S(1)}, f32[16,2048]{1,0:T(8,128)S(1)}, u32[]{:S(2)}, u32[]{:S(2)}) collective-permute-start(f32[16,2048]{1,0:T(8,128)S(1)} %convert_reduce_fusion), channel_id=1, source_target_pairs={{0,24},{4,28},{8,0},{12,4},{16,8},{20,12},{24,16},{28,20},{1,25},{... | collective-permute-start | bytes 393224 | tf_op jit(solution)/shard_map/ppermute | solution.py:189
  23.9 10.9 %collective-permute-start.2 = (f32[16,2048]{1,0:T(8,128)S(1)}, f32[16,2048]{1,0:T(8,128)}, u32[]{:S(2)}, u32[]{:S(2)}) collective-permute-start(f32[16,2048]{1,0:T(8,128)S(1)} %convert_reduce_fusion), channel_id=1, source_target_pairs={{0,16},{4,20},{8,24},{12,28},{16,0},{20,4},{24,8},{28,12},{1,17},{... | collective-permute-start | bytes 393224 | tf_op jit(solution)/shard_map/ppermute | solution.py:189
  23.9 10.9 %collective-permute-start.1 = (f32[16,2048]{1,0:T(8,128)S(1)}, f32[16,2048]{1,0:T(8,128)}, u32[]{:S(2)}, u32[]{:S(2)}) collective-permute-start(f32[16,2048]{1,0:T(8,128)S(1)} %convert_reduce_fusion), channel_id=1, source_target_pairs={{0,8},{4,12},{8,16},{12,20},{16,24},{20,28},{24,0},{28,4},{1,9},{5... | collective-permute-start | bytes 393224 | tf_op jit(solution)/shard_map/ppermute | solution.py:189
  27.8 0.7 copy-start.9
  27.8 18.9 %collective-permute-start.6 = (bf16[512,8,128]{2,1,0:T(8,128)(2,1)S(1)}, bf16[512,8,128]{2,1,0:T(8,128)(2,1)}, u32[]{:S(2)}, u32[]{:S(2)}) collective-permute-start(bf16[512,8,128]{2,1,0:T(8,128)(2,1)S(1)} %bitcast.70), channel_id=1, source_target_pairs={{0,1},{1,0},{2,3},{3,2},{4,5},{5,4},{6,7},{7,6},{8,9},{9,8},{10,11... | collective-permute-start | bytes 3145736 | tf_op jit(solution)/shard_map/ppermute | solution.py:204
  28.5 18.2 %collective-permute-start.7 = (bf16[512,8,128]{2,1,0:T(8,128)(2,1)S(1)}, bf16[512,8,128]{2,1,0:T(8,128)(2,1)}, u32[]{:S(2)}, u32[]{:S(2)}) collective-permute-start(bf16[512,8,128]{2,1,0:T(8,128)(2,1)S(1)} %collective-permute-done.5.refs_1_), channel_id=1, source_target_pairs={{0,1},{1,0},{2,3},{3,2},{4,5},{5,4},{6,7},{7,6},{8,9},{9,8},{10,11... | collective-permute-start | bytes 3145736 | tf_op jit(solution)/shard_map/ppermute | solution.py:204
  35.9 5.0 %collective-permute-start.4 = (f32[16,2048]{1,0:T(8,128)S(1)}, f32[16,2048]{1,0:T(8,128)S(1)}, u32[]{:S(2)}, u32[]{:S(2)}) collective-permute-start(f32[16,2048]{1,0:T(8,128)S(1)} %add_add_fusion), channel_id=1, source_target_pairs={{0,4},{4,0},{8,12},{12,8},{16,20},{20,16},{24,28},{28,24},{1,5},{5... | collective-permute-start | bytes 393224 | tf_op jit(solution)/shard_map/ppermute | solution.py:185
  74.2 1.9 %copy-start.2 = (f32[384,8,128]{2,1,0:T(8,128)S(1)}, f32[384,8,128]{2,1,0:T(8,128)}, u32[]{:S(2)}) copy-start(f32[384,8,128]{2,1,0:T(8,128)} %get-tuple-element.11) | copy-start | bytes 4718596
  77.5 10.2 %collective-permute-start.8 = (s16[416,256]{1,0:T(8,128)(2,1)}, s16[416,256]{1,0:T(8,128)(2,1)}, u32[]{:S(2)}, u32[]{:S(2)}) collective-permute-start(s16[416,256]{1,0:T(8,128)(2,1)} %get-tuple-element.29), channel_id=1, source_target_pairs={{0,8},{4,12},{8,16},{12,20},{16,24},{20,28},{24,0},{28,4},{1,9},{5... | collective-permute-start | bytes 638984 | tf_op jit(solution)/shard_map/ppermute | solution.py:189
  78.3 0.9 copy-start.8
  78.4 4.0 %copy-start.7 = (s16[416,256]{1,0:T(8,128)(2,1)S(1)}, s16[416,256]{1,0:T(8,128)(2,1)}, u32[]{:S(2)}) copy-start(s16[416,256]{1,0:T(8,128)(2,1)} %get-tuple-element.31) | copy-start | bytes 638980
  79.3 10.3 %collective-permute-start.10 = (s16[416,256]{1,0:T(8,128)(2,1)S(1)}, s16[416,256]{1,0:T(8,128)(2,1)S(1)}, u32[]{:S(2)}, u32[]{:S(2)}) collective-permute-start(s16[416,256]{1,0:T(8,128)(2,1)S(1)} %copy-done.8), channel_id=1, source_target_pairs={{0,24},{4,28},{8,0},{12,4},{16,8},{20,12},{24,16},{28,20},{1,25},{... | collective-permute-start | bytes 638984 | tf_op jit(solution)/shard_map/ppermute | solution.py:189
  82.4 16.4 %collective-permute-start.9 = (s16[416,256]{1,0:T(8,128)(2,1)S(1)}, s16[416,256]{1,0:T(8,128)(2,1)S(1)}, u32[]{:S(2)}, u32[]{:S(2)}) collective-permute-start(s16[416,256]{1,0:T(8,128)(2,1)S(1)} %copy-done.7), channel_id=1, source_target_pairs={{0,16},{4,20},{8,24},{12,28},{16,0},{20,4},{24,8},{28,12},{1,17},{... | collective-permute-start | bytes 638984 | tf_op jit(solution)/shard_map/ppermute | solution.py:189
  107.2 16.0 %copy-start.5 = (f32[16,2048]{1,0:T(8,128)S(1)}, f32[16,2048]{1,0:T(8,128)}, u32[]{:S(2)}) copy-start(f32[16,2048]{1,0:T(8,128)} %add.242) | copy-start | bytes 393220
  126.6 19.9 %collective-permute-start.11 = (s16[4,48,2176]{2,1,0:T(8,128)(2,1)}, s16[4,48,2176]{2,1,0:T(8,128)(2,1)}, u32[]{:S(2)}, u32[]{:S(2)}) collective-permute-start(s16[4,48,2176]{2,1,0:T(8,128)(2,1)} %pad_add_fusion.2), channel_id=1, source_target_pairs={{0,4},{4,0},{8,12},{12,8},{16,20},{20,16},{24,28},{28,24},{1,5},{5... | collective-permute-start | bytes 2506760 | tf_op jit(solution)/shard_map/ppermute | solution.py:185
  149.1 1.2 copy-start.3
  150.6 9.9 %collective-permute-start.12 = (s16[48,2176]{1,0:T(8,128)(2,1)S(1)}, s16[48,2176]{1,0:T(8,128)(2,1)S(1)}, u32[]{:S(2)}, u32[]{:S(2)}) collective-permute-start(s16[48,2176]{1,0:T(8,128)(2,1)S(1)} %get-tuple-element.32), channel_id=1, source_target_pairs={{0,8},{4,12},{8,16},{12,20},{16,24},{20,28},{24,0},{28,4},{1,9},{5... | collective-permute-start | bytes 626696 | tf_op jit(solution)/shard_map/ppermute | solution.py:189
  150.7 16.1 %collective-permute-start.13 = (s16[48,2176]{1,0:T(8,128)(2,1)S(1)}, s16[48,2176]{1,0:T(8,128)(2,1)S(1)}, u32[]{:S(2)}, u32[]{:S(2)}) collective-permute-start(s16[48,2176]{1,0:T(8,128)(2,1)S(1)} %get-tuple-element.33), channel_id=1, source_target_pairs={{0,16},{4,20},{8,24},{12,28},{16,0},{20,4},{24,8},{28,12},{1,17},{... | collective-permute-start | bytes 626696 | tf_op jit(solution)/shard_map/ppermute | solution.py:189
  152.2 14.7 %collective-permute-start.14 = (s16[48,2176]{1,0:T(8,128)(2,1)S(1)}, s16[48,2176]{1,0:T(8,128)(2,1)S(1)}, u32[]{:S(2)}, u32[]{:S(2)}) collective-permute-start(s16[48,2176]{1,0:T(8,128)(2,1)S(1)} %get-tuple-element.34), channel_id=1, source_target_pairs={{0,24},{4,28},{8,0},{12,4},{16,8},{20,12},{24,16},{28,20},{1,25},{... | collective-permute-start | bytes 626696 | tf_op jit(solution)/shard_map/ppermute | solution.py:189

commit v2 on v1

--- a/solution.py
+++ b/solution.py
@@ -1,4 +1,3 @@
-import functools
 import math
 
 import jax
@@ -7,6 +6,7 @@
 from jax.experimental import pallas as pl
 from jax.experimental.pallas import tpu as pltpu
 from jax.sharding import PartitionSpec as P
+
 
 discount = 0.95
 LANES = 128
@@ -63,12 +63,14 @@
     return jnp.concatenate(cuts, axis=-1)
 
 
-def selecting_kernel(depth, act_ref, idx_ref, kept_ref, got_ref, *refs):
+def selecting_kernel(act_ref, own_idx_ref, got_idx_ref, kept_ref, got_ref, *refs):
     *pieces, out_ref, totals_ref, table, w_table, inverse = refs
     rows, half = out_ref.shape[0], out_ref.shape[1] * out_ref.shape[2]
     tile = out_ref.shape[1]
     actions = totals_ref.shape[0]
     kept_rows = kept_ref.shape[0]
+    near = kept_rows // actions
+    depth = 2 * near
 
     @pl.when(pl.program_id(0) == 0)
     def _():
@@ -106,14 +108,16 @@
         inverse[...] = (1.0 / total).reshape(actions * tile, LANES)
 
     first = pl.program_id(0) * rows
+    span = own_idx_ref.shape[0] - near + 1
+    spots = [ref.at[pl.ds(o, span)] for ref in (own_idx_ref, got_idx_ref) for o in range(near)]
 
     def one(row, carry):
         kind = act_ref[first + row]
         at = pl.multiple_of(kind * (depth * tile), depth * tile)
-        listed = idx_ref.at[pl.ds((first + row) * depth, depth)]
+        listed = (first + row) * near
         parts = []
         for o in range(depth):
-            place = pl.multiple_of(listed[o], tile)
+            place = pl.multiple_of(spots[o][listed], tile)
             term = w_table[pl.ds(at + o * tile, tile)] * table[pl.ds(place, tile)]
             if o < 4:
                 parts.append(term)
@@ -128,19 +132,21 @@
     lax.fori_loop(0, rows, one, 0, unroll=4)
 
 
-def select_and_sum(actions, picks, kept, got, pieces, count, kinds):
+def select_and_sum(actions, own_picks, got_picks, kept, got, pieces, kinds):
     half = kept.shape[1]
-    depth = picks.shape[0] // count
+    count = actions.shape[0]
+    depth = 2 * kept.shape[0] // kinds
     tiles = pieces[0].shape[1:]
     step = math.gcd(count, 32)
     known = sum(piece.shape[0] for piece in pieces)
     whole = [pl.BlockSpec(memory_space=pltpu.VMEM) for _ in range(2 + len(pieces))]
     return pl.pallas_call(
-        functools.partial(selecting_kernel, depth),
+        selecting_kernel,
         grid=(count // step,),
         in_specs=[
             pl.BlockSpec(memory_space=pltpu.SMEM),
             pl.BlockSpec(memory_space=pltpu.SMEM),
+            pl.BlockSpec(memory_space=pltpu.SMEM),
             *whole,
         ],
         out_specs=[
@@ -160,10 +166,56 @@
             dimension_semantics=("arbitrary",), vmem_limit_bytes=48 * 1024 * 1024
         ),
         name="select_and_sum",
-    )(actions, picks, kept, got, *pieces)
-
-
-def body(alpha_set, transitions, obs_weights, rewards, chosen_idx, chosen_action):
+    )(actions, own_picks, got_picks, kept, got, *pieces)
+
+
+def moving_kernel(kinds_ref, halves_ref, trans_ref, inverse_ref, out_ref, spread):
+    rows = out_ref.shape[0]
+    actions, width, columns = trans_ref.shape
+
+    @pl.when(pl.program_id(0) == 0)
+    def _():
+        for kind in range(actions):
+            held = jnp.where(kinds_ref[...] == kind, halves_ref[...], 0.0)
+            spread[:, kind * width : (kind + 1) * width] = held.astype(jnp.bfloat16)
+
+    product = jnp.dot(
+        spread[...], trans_ref[...].reshape(actions * width, columns), preferred_element_type=jnp.float32
+    )
+    kinds = lax.broadcasted_iota(jnp.int32, (rows, actions), 1)
+    hot = (kinds_ref[:rows] == kinds).astype(jnp.float32)
+    factor = jnp.dot(
+        hot, inverse_ref[...], precision=lax.Precision.HIGHEST, preferred_element_type=jnp.float32
+    )
+    out_ref[...] = (product[:rows] + product[rows:]) * factor
+
+
+def move(kinds, weighted, transitions, inverse):
+    rows, width = weighted.shape
+    actions, _, states = transitions.shape
+    upper = lax.reduce_precision(weighted, 8, 7)
+    halves = jnp.concatenate([upper, weighted - upper])
+    columns = math.gcd(states, 512)
+    return pl.pallas_call(
+        moving_kernel,
+        grid=(states // columns,),
+        in_specs=[
+            pl.BlockSpec(memory_space=pltpu.VMEM),
+            pl.BlockSpec(memory_space=pltpu.VMEM),
+            pl.BlockSpec((actions, width, columns), lambda n: (0, 0, n)),
+            pl.BlockSpec((actions, columns), lambda n: (0, n)),
+        ],
+        out_specs=pl.BlockSpec((rows, columns), lambda n: (0, n)),
+        out_shape=jax.ShapeDtypeStruct((rows, states), jnp.float32),
+        scratch_shapes=[pltpu.VMEM((2 * rows, actions * width), jnp.bfloat16)],
+        compiler_params=pltpu.CompilerParams(
+            dimension_semantics=("arbitrary",), vmem_limit_bytes=48 * 1024 * 1024
+        ),
+        name="move",
+    )(jnp.concatenate([kinds, kinds])[:, None], halves, transitions, inverse)
+
+
+def backup(alpha_set, transitions, obs_weights, rewards, chosen_idx, chosen_action):
     actions, states = rewards.shape
     obs_local = obs_weights.shape[0]
     bel_rows = chosen_action.shape[0]
@@ -208,36 +260,29 @@
     action_hot = (chosen_action[:, None] == jnp.arange(actions, dtype=jnp.int32)[None, :])
     picks = jnp.sum(jnp.where(action_hot[:, :, None], chosen_idx, 0), axis=1)
     action_hot = action_hot.astype(jnp.float32)
-
-    kept = columns_of(obs_weights, inner_at, inner, outer).reshape(obs_local * actions, half)
-    given = log_code(columns_of(obs_weights, 1 - inner_at, inner, outer), 1.0)
-    given = given.reshape(obs_local * actions, half)
-    listed = picks.astype(jnp.int16).reshape(-1)
-    pad = -listed.shape[0] % (16 * half)
-    listed_rows = jnp.pad(listed, (0, pad)).reshape(-1, half)
-    got = swap_inner(jnp.concatenate([given, listed_rows], axis=0))
-    got_picks = got[obs_local * actions :].reshape(-1)[: listed.shape[0]].astype(jnp.int32).reshape(bel_rows, obs_local)
-
-    share = jnp.sum(transitions.astype(jnp.float32), axis=1)
-    if outer <= DIRECT:
-        trans_totals = share
-        for k in range(1, outer):
-            trans_totals = trans_totals + shift_outer(share, k)
-        trans_totals = trans_totals + swap_inner(trans_totals)
-    else:
-        trans_totals = lax.psum(share, "obs")
-
-    both_picks = jnp.concatenate([picks, got_picks], axis=1)
-    block, inside = both_picks // known_local, lax.rem(both_picks, known_local)
-    relative = block ^ seat
+    relative = (picks // known_local) ^ seat
     place = jnp.zeros_like(relative)
     for at, member in enumerate(order):
         place = jnp.where(relative == member, at, place)
-    rows = (place * known_local + inside) * tiles[0]
-    rows, trans_totals = lax.optimization_barrier((rows, trans_totals))
-    shares, here_totals = select_and_sum(
-        chosen_action, rows.reshape(-1), kept, got, pieces, bel_rows, actions
-    )
+    own_rows = ((place * known_local + lax.rem(picks, known_local)) * tiles[0]).reshape(-1)
+    got_rows = swap_inner(own_rows)
+
+    kept = columns_of(obs_weights, inner_at, inner, outer).reshape(obs_local * actions, half)
+    given = log_code(columns_of(obs_weights, 1 - inner_at, inner, outer), 1.0)
+    given, late = lax.optimization_barrier((given.reshape(obs_local * actions, half), transitions))
+    got = swap_inner(given)
+
+    share = jnp.sum(late.astype(jnp.float32), axis=1)
+    if outer <= DIRECT:
+        column_share = share
+        for k in range(1, outer):
+            column_share = column_share + shift_outer(share, k)
+        own_rows, column_share = lax.optimization_barrier((own_rows, column_share))
+        trans_totals = column_share + swap_inner(column_share)
+    else:
+        trans_totals = lax.psum(share, "obs")
+
+    shares, here_totals = select_and_sum(chosen_action, own_rows, got_rows, kept, got, pieces, actions)
     shares = shares.reshape(bel_rows, half)
 
     power, code = step_code(shares, 0)
@@ -257,25 +302,34 @@
         above, below = above + factor * part, below + factor
     weighted = above / below
 
-    upper = lax.reduce_precision(weighted, 8, 7)
-    lower = weighted - upper
-    halves = jnp.stack([upper, lower]).astype(jnp.bfloat16)
-    spread = (action_hot.astype(jnp.bfloat16)[None, :, :, None] * halves[:, :, None, :]).reshape(
-        2 * bel_rows, actions * width
-    )
-    moved = jnp.dot(
-        spread, transitions.reshape(actions * width, states), preferred_element_type=jnp.float32
-    )
-    inverse = jnp.dot(action_hot, 1.0 / trans_totals, precision=lax.Precision.HIGHEST)
-    future = (moved[:bel_rows] + moved[bel_rows:]) * inverse
-
-    future = future.reshape(outer, inner, owned, states)
-    ours = lax.dynamic_index_in_dim(future, inner_at, 1, keepdims=False)
-    theirs = lane_code(lax.dynamic_index_in_dim(future, 1 - inner_at, 1, keepdims=False))
-    ours = ours + lane_value(swap_inner(theirs), states)
-    coded = lane_code(ours)
-    total = lax.dynamic_index_in_dim(ours, outer_at, 0, keepdims=False)
-    for block in exchange_outer(lambda q: lax.dynamic_index_in_dim(coded, q, 0, keepdims=False)):
+    def rows_of(array, at):
+        array = array.reshape((outer, inner, owned) + array.shape[1:])
+        array = lax.dynamic_index_in_dim(array, at, 1, keepdims=False)
+        array = lax.dynamic_slice_in_dim(jnp.concatenate([array, array]), outer_at, outer, 0)
+        return array.reshape((outer * owned,) + array.shape[2:])
+
+    inverse = 1.0 / trans_totals
+    theirs = lane_code(
+        move(rows_of(chosen_action, 1 - inner_at), rows_of(weighted, 1 - inner_at), transitions, inverse)
+    )
+    ours = move(rows_of(chosen_action, inner_at), rows_of(weighted, inner_at), transitions, inverse)
+    cut = outer // 2
+    far = swap_inner(theirs[cut * owned :])
+    near = swap_inner(theirs[: cut * owned])
+    far = lane_code(ours[cut * owned :] + lane_value(far, states))
+    if outer <= DIRECT:
+        blocks = [shift_outer(far[k * owned : (k + 1) * owned], cut + k) for k in range(outer - cut)]
+        total = ours[:owned] + lane_value(near[:owned], states)
+        near = lane_code(ours[owned : cut * owned] + lane_value(near[owned:], states))
+        blocks += [shift_outer(near[k * owned : (k + 1) * owned], 1 + k) for k in range(cut - 1)]
+    else:
+        near = ours[: cut * owned] + lane_value(near, states)
+        total = near[:owned]
+        coded = jnp.concatenate([lane_code(near), far]).reshape(outer, owned, -1)
+        blocks = exchange_outer(
+            lambda q: lax.dynamic_index_in_dim(coded, lax.rem(q - outer_at + outer, outer), 0, keepdims=False)
+        )
+    for block in blocks:
         total = total + lane_value(block, states)
     own_hot = lax.dynamic_slice_in_dim(action_hot, me * owned, owned, 0)
     reward_rows = jnp.dot(own_hot, rewards, precision=lax.Precision.HIGHEST)
@@ -291,6 +345,4 @@
         P("bel", None, "obs"),
         P("bel"),
     )
-    return jax.shard_map(
-        body, mesh=mesh, in_specs=placed, out_specs=P(("bel", "obs"), None), check_vma=False
-    )
+    return jax.shard_map(backup, mesh=mesh, in_specs=placed, out_specs=P(("bel", "obs"), None), check_vma=False)

time: 172 us -> 149 us (0.87); the launches traced: 169 us -> 149 us
  Pallas kernels: 27.6 us -> 48.2 us
  matrix products: 21 us -> 2.27 us
  local copies, waits for them, and re-layouts: 18.8 us -> 7.83 us
  waiting for transfers between devices: 56.7 us -> 46.9 us
  other arithmetic: 25.7 us -> 20.8 us
  starting transfers between devices: 19.3 us -> 22.3 us
    pallas_call x1 -> x3, Pallas kernels: 27.6 us -> 48.2 us  [the longest x1 24.9 us: select_and_sum(): pl.pallas_call(selecting_kernel, grid=(count // step,), in_specs=[pl.Bloc...]
    dot_general x4 -> x2, matrix products: 21 us -> 2.27 us  [the longest x1 1.45 us: backup(): reward_rows = jnp.dot(own_hot, rewards, precision=lax.Precision.HIGHEST)]
    unnamed x27 -> x8, local copies, waits for them, and re-layouts: 8.42 us -> 0.8 us
    ppermute x3 -> x5, waiting for transfers between devices: 20.1 us -> 14.1 us  [swap_inner(): return lax.ppermute(array, 'obs', [(i, i ^ 1) for i in range(ranks)])]
    ppermute x9, waiting for transfers between devices: 36.4 us -> 31.1 us  [shift_outer(): return lax.ppermute(array, 'obs', hops)]
    ppermute x3 -> x5, starting transfers between devices: 3.22 us -> 6.7 us  [swap_inner(): return lax.ppermute(array, 'obs', [(i, i ^ 1) for i in range(ranks)])]
    convert_element_type x5 -> x0, local copies, waits for them, and re-layouts: 2.08 us -> none  [the longest x2 1.67 us: body(): got[obs_local * actions:].reshape(-1)[:listed.shape[0]].astype(jnp.int32)]
    reduce_sum x2, other arithmetic: 7.06 us -> 8.83 us  [the longest x1 7.62 us: backup(): share = jnp.sum(late.astype(jnp.float32), axis=1)]
  transfers between devices with their start and end apart: 15 -> 17, of which waited for: 10 -> 9; matrix products, arithmetic and copies ran while one was open for 14% -> 17% of each run, Pallas kernels for 0% -> 25%
where the time goes in v2:
time: 149 us
  Pallas kernels  48.2 us (32%)
  waiting for transfers between devices  46.9 us (31%)
  starting transfers between devices  22.3 us (15%)
  other arithmetic  20.8 us (14%)
  local copies, waits for them, and re-layouts  7.83 us (5%)
  matrix products  2.27 us (2%)
    ppermute x9, waiting for transfers between devices, shift_outer(): return lax.ppermute(array, 'obs', hops)  31.1 us
    pallas_call x1, Pallas kernels, select_and_sum(): pl.pallas_call(selecting_kernel, grid=(count // step,), in_specs=[pl.Bloc...  24.9 us
    pallas_call x2, Pallas kernels, move(): pl.pallas_call(moving_kernel, grid=(states // columns,), in_specs=[pl.Blo...  23.3 us
    ppermute x5, waiting for transfers between devices, swap_inner(): return lax.ppermute(array, 'obs', [(i, i ^ 1) for i in range(ranks)])  14.1 us
    ppermute x9, starting transfers between devices, shift_outer(): return lax.ppermute(array, 'obs', hops)  12.6 us
    reduce_sum x1, other arithmetic, backup(): share = jnp.sum(late.astype(jnp.float32), axis=1)  7.62 us
    ppermute x5, starting transfers between devices, swap_inner(): return lax.ppermute(array, 'obs', [(i, i ^ 1) for i in range(ranks)])  6.7 us
    dynamic_slice x2, local copies, waits for them, and re-layouts, columns_of(): lax.dynamic_slice_in_dim(array, (place * inner + inner_at) * width, width...  5.31 us
  transfers between devices with their start and end apart: 17, of which 9 were waited for; matrix products, arithmetic and copies ran while one was open for 17% of the time, Pallas kernels for 25%

profile of v2, /device:TPU:0, one launch (start us, length us, event | category | flops | bytes accessed | tf_op | source)
XLA Modules:
  0.0 148.8 jit_solution(11228538500312107617)
XLA Ops:
  0.0 1.3 constant_dynamic-slice_fusion.9
  1.3 0.1 maximum_bitcast_fusion
  1.4 0.3 copy.15
  1.7 3.1 %collective-permute-start.5 = (bf16[512,8,128]{2,1,0:T(8,128)(2,1)S(1)}, bf16[512,8,128]{2,1,0:T(8,128)(2,1)S(1)}, u32[]{:S(2)}, u32[]{:S(2)}) collective-permute-start(bf16[512,8,128]{2,1,0:T(8,128)(2,1)S(1)} %bitcast.39), channel_id=1, source_target_pairs={{0,2},{1,3},{2,0},{3,1},{4,6},{5,7},{6,4},{7,5},{8,10},{9,11},{10,... | collective-permute-start | bytes 3145736 | tf_op jit(solution)/shard_map/ppermute | solution.py:256
  4.8 4.0 %constant_dynamic-slice_fusion.13 = (f32[32,16,256]{2,1,0:T(8,128)}, f32[32,16,256]{2,1,0:T(8,128)}, f32[32,16,256]{2,1,0:T(8,128)S(1)}, f32[32,16,256]{2,1,0:T(...) fusion(f32[32,16,2048]{2,1,0:T(8,128)} %param.8, ...), kind=kLoop, calls=%fused_computation.98 | loop fusion | bytes 8388640 | tf_op jit(solution)/shard_map/dynamic_slice | solution.py:60
  8.8 1.7 %fusion.7 = s16[512,1024]{1,0:T(8,128)(2,1)} fusion(f32[512,256]{1,0:T(8,128)S(1)} %bitcast.46, f32[512,256]{1,0:T(8,128)S(1)} %bitcast.47, f32[512,256]{1,0:T(8,128)S(1)} %bitcast.48, f32[512,256]{1,0:T(8,128)S(1)} %bitcast.49), kind=kLoop, calls=%fused_computation.10 | loop fusion | flops 5767168 | bytes 3145728 | tf_op jit(solution)/shard_map/convert_element_type | solution.py:22
  10.5 7.6 %convert_reduce_fusion = f32[16,2048]{1,0:T(8,128)} fusion(bf16[16,256,2048]{2,1,0:T(8,128)(2,1)} %trans_ref.3), kind=kLoop, calls=%fused_computation | loop fusion | flops 16744448 | bytes 16908288 | tf_op jit(solution)/shard_map/reduce_sum | solution.py:275
  18.1 3.6 %collective-permute-start.2 = (f32[16,2048]{1,0:T(8,128)}, f32[16,2048]{1,0:T(8,128)}, u32[]{:S(2)}, u32[]{:S(2)}) collective-permute-start(f32[16,2048]{1,0:T(8,128)} %convert_reduce_fusion), channel_id=1, source_target_pairs={{0,24},{4,28},{8,0},{12,4},{16,8},{20,12},{24,16},{28,20},{1,25},{... | collective-permute-start | bytes 393224 | tf_op jit(solution)/shard_map/ppermute | solution.py:241
  21.7 1.5 %collective-permute-start.4 = (s16[512,1024]{1,0:T(8,128)(2,1)}, s16[512,1024]{1,0:T(8,128)(2,1)}, u32[]{:S(2)}, u32[]{:S(2)}) collective-permute-start(s16[512,1024]{1,0:T(8,128)(2,1)} %fusion.7), channel_id=1, source_target_pairs={{0,4},{4,0},{8,12},{12,8},{16,20},{20,16},{24,28},{28,24},{1,5},{5... | collective-permute-start | bytes 3145736 | tf_op jit(solution)/shard_map/ppermute | solution.py:237
  23.2 0.1 reshape.165
  23.3 1.2 select_reduce_fusion
  24.5 0.1 copy.12
  24.7 0.7 reduce_sum.21
  25.4 0.9 add_multiply_fusion.own_idx_ref
  26.3 1.7 %collective-permute-done.5.refs_1_ = bf16[512,8,128]{2,1,0:T(8,128)(2,1)S(1)} collective-permute-done((bf16[512,8,128]{2,1,0:T(8,128)(2,1)S(1)}, bf16[512,8,128]{2,1,0:T(8,128)(2,1)S(1)}, u32[]{:S(2)}, u32[]{:S(2)}) %collective-permute-start.5) | collective-permute-done | bytes 1048608 | tf_op jit(solution)/shard_map/ppermute | solution.py:256
  28.0 0.1 reshape.166
  28.1 0.1 reshape.172
  28.2 0.1 pad_add_fusion.7
  28.3 0.1 broadcast_in_dim.62.kinds_ref
  28.4 1.8 %collective-permute-start = (f32[16,2048]{1,0:T(8,128)}, f32[16,2048]{1,0:T(8,128)S(1)}, u32[]{:S(2)}, u32[]{:S(2)}) collective-permute-start(f32[16,2048]{1,0:T(8,128)} %convert_reduce_fusion), channel_id=1, source_target_pairs={{0,8},{4,12},{8,16},{12,20},{16,24},{20,28},{24,0},{28,4},{1,9},{5... | collective-permute-start | bytes 393224 | tf_op jit(solution)/shard_map/ppermute | solution.py:241
  30.3 3.1 %pad_maximum_fusion = f32[32,16,1024]{2,1,0:T(8,128)} fusion(f32[32,16,256]{2,1,0:T(8,128)} %get-tuple-element.25, f32[32,16,256]{2,1,0:T(8,128)} %get-tuple-element.26, f32[32,16,256]{2,1,0:T(8,128)} %get-tuple-element.20, f32[32,16,256]{2,1,0:T(8,128)} %get-tuple-element.19), kind=kLoop, calls=%fused_computation.11 | loop fusion | flops 1572864 | bytes 4194304 | tf_op jit(solution)/shard_map/concatenate | solution.py:63
  33.4 1.5 %collective-permute-start.3 = (s32[12288]{0:T(1024)S(1)}, s32[12288]{0:T(1024)S(1)}, u32[]{:S(2)}, u32[]{:S(2)}) collective-permute-start(s32[12288]{0:T(1024)S(1)} %add_multiply_fusion.own_idx_ref), channel_id=1, source_target_pairs={{0,4},{4,0},{8,12},{12,8},{16,20},{20,16},{24,28},{28,24},{1,5},{5... | collective-permute-start | bytes 147464 | tf_op jit(solution)/shard_map/ppermute | solution.py:237
  34.9 1.8 %collective-permute-done = f32[16,2048]{1,0:T(8,128)S(1)} collective-permute-done((f32[16,2048]{1,0:T(8,128)}, f32[16,2048]{1,0:T(8,128)S(1)}, u32[]{:S(2)}, u32[]{:S(2)}) %collective-permute-start) | collective-permute-done | bytes 131104 | tf_op jit(solution)/shard_map/ppermute | solution.py:241
  36.7 1.1 add_add_fusion
  37.7 1.6 %collective-permute-start.11 = (f32[16,2048]{1,0:T(8,128)S(1)}, f32[16,2048]{1,0:T(8,128)S(1)}, u32[]{:S(2)}, u32[]{:S(2)}) collective-permute-start(f32[16,2048]{1,0:T(8,128)S(1)} %add_add_fusion), channel_id=1, source_target_pairs={{0,4},{4,0},{8,12},{12,8},{16,20},{20,16},{24,28},{28,24},{1,5},{5... | collective-permute-start | bytes 393224 | tf_op jit(solution)/shard_map/ppermute | solution.py:237
  39.3 9.7 %collective-permute-done.3.got_idx_ref = s32[12288]{0:T(1024)S(1)} collective-permute-done((s32[12288]{0:T(1024)S(1)}, s32[12288]{0:T(1024)S(1)}, u32[]{:S(2)}, u32[]{:S(2)}) %collective-permute-start.3) | collective-permute-done | bytes 49184 | tf_op jit(solution)/shard_map/ppermute | solution.py:237
  49.0 24.9 %select_and_sum.1 = (f32[384,8,128]{2,1,0:T(8,128)}, f32[16,1024]{1,0:T(8,128)S(1)}) custom-call(s32[384]{0:T(512)S(1)} %copy-done.1, s32[12288]{0:T(1024)S(1)} %add_multiply_fusion.own_idx_ref, s32[12288]{0:T(1024)S(1)} %collective-permute-done.3.got_idx_ref, f32[512,1024]{1,0:T(8,128)} %bitcast.44, s16[512,1024]{1,0:T(8,128)(2,1)} %collective-permute-done.4.got_ref, ...), custom_call_target="tpu_custom_call" | custom-call | tf_op jit(solution)/shard_map/select_and_sum/pallas_call | solution.py:143
  73.9 1.6 %abs_reduce_fusion.1 = f32[8,128]{1,0:T(8,128)S(1)} fusion(f32[384,8,128]{2,1,0:T(8,128)} %get-tuple-element.15), kind=kLoop, calls=%fused_computation.16 | loop fusion | flops 785408 | bytes 1576960 | tf_op jit(solution)/shard_map/reduce_max | solution.py:31
  75.6 0.2 copy-done.2
  75.8 0.4 convert_convert_fusion.1
  76.3 0.1 constant_dynamic-slice_fusion.4
  76.4 0.8 collective-permute-start.10
  77.2 0.3 copy.20
  77.6 2.2 %collective-permute-start.9 = (s16[416,256]{1,0:T(8,128)(2,1)S(1)}, s16[416,256]{1,0:T(8,128)(2,1)S(1)}, u32[]{:S(2)}, u32[]{:S(2)}) collective-permute-start(s16[416,256]{1,0:T(8,128)(2,1)S(1)} %get-tuple-element.33), channel_id=1, source_target_pairs={{0,16},{4,20},{8,24},{12,28},{16,0},{20,4},{24,8},{28,12},{1,17},{... | collective-permute-start | bytes 638984 | tf_op jit(solution)/shard_map/ppermute | solution.py:241
  79.8 2.0 %collective-permute-start.8 = (s16[416,256]{1,0:T(8,128)(2,1)S(1)}, s16[416,256]{1,0:T(8,128)(2,1)S(1)}, u32[]{:S(2)}, u32[]{:S(2)}) collective-permute-start(s16[416,256]{1,0:T(8,128)(2,1)S(1)} %get-tuple-element.31), channel_id=1, source_target_pairs={{0,8},{4,12},{8,16},{12,20},{16,24},{20,28},{24,0},{28,4},{1,9},{5... | collective-permute-start | bytes 638984 | tf_op jit(solution)/shard_map/ppermute | solution.py:241
  81.8 1.3 collective-permute-done.10
  83.1 14.5 %collective-permute-done.9 = s16[416,256]{1,0:T(8,128)(2,1)S(1)} collective-permute-done((s16[416,256]{1,0:T(8,128)(2,1)S(1)}, s16[416,256]{1,0:T(8,128)(2,1)S(1)}, u32[]{:S(2)}, u32[]{:S(2)}) %collective-permute-start.9) | collective-permute-done | bytes 213024 | tf_op jit(solution)/shard_map/ppermute | solution.py:241
  97.7 0.8 fusion.16
  98.6 0.4 add_divide_fusion
  99.0 0.1 fusion.14
  99.1 11.7 %move.3 = f32[192,2048]{1,0:T(8,128)S(1)} custom-call(s32[384,1]{1,0:T(8,128)S(1)} %broadcast_in_dim.62.kinds_ref, f32[384,256]{1,0:T(8,128)S(1)} %pad_maximum_fusion.2.halves_ref, bf16[16,256,2048]{2,1,0:T(8,128)(2,1)} %trans_ref.3, f32[16,2048]{1,0:T(8,128)S(1)} %add_divide_fusion.1.inverse_ref), custom_call_target="tpu_custom_call" | custom-call | tf_op jit(solution)/shard_map/move/pallas_call | solution.py:199
  110.8 0.2 abs_reduce_fusion
  111.0 0.3 convert_convert_fusion
  111.3 0.1 broadcast_in_dim.58
  111.4 1.6 %collective-permute-start.12 = (s16[96,2176]{1,0:T(8,128)(2,1)S(1)}, s16[96,2176]{1,0:T(8,128)(2,1)S(1)}, u32[]{:S(2)}, u32[]{:S(2)}) collective-permute-start(s16[96,2176]{1,0:T(8,128)(2,1)S(1)} %get-tuple-element.35), channel_id=1, source_target_pairs={{0,4},{4,0},{8,12},{12,8},{16,20},{20,16},{24,28},{28,24},{1,5},{5... | collective-permute-start | bytes 1253384 | tf_op jit(solution)/shard_map/ppermute | solution.py:237
  113.0 0.1 pad_add_fusion.6
  113.1 0.1 broadcast_in_dim.61.kinds_ref
  113.2 0.6 collective-permute-start.13
  113.9 11.7 %move.2 = f32[192,2048]{1,0:T(8,128)S(1)} custom-call(s32[384,1]{1,0:T(8,128)S(1)} %broadcast_in_dim.61.kinds_ref, f32[384,256]{1,0:T(8,128)S(1)} %pad_maximum_fusion.1.halves_ref, bf16[16,256,2048]{2,1,0:T(8,128)(2,1)} %trans_ref.3, f32[16,2048]{1,0:T(8,128)S(1)} %add_divide_fusion.1.inverse_ref), custom_call_target="tpu_custom_call" | custom-call | tf_op jit(solution)/shard_map/move/pallas_call | solution.py:199
  125.5 0.1 multiply_reduce_fusion.5
  125.7 0.2 abs_reduce_fusion.3
  125.9 0.2 convert_convert_fusion.3
  126.2 4.4 %collective-permute-done.13 = s16[96,2176]{1,0:T(8,128)(2,1)S(1)} collective-permute-done((s16[96,2176]{1,0:T(8,128)(2,1)S(1)}, s16[96,2176]{1,0:T(8,128)(2,1)S(1)}, u32[]{:S(2)}, u32[]{:S(2)}) %collective-permute-start.13) | collective-permute-done | bytes 417824 | tf_op jit(solution)/shard_map/ppermute | solution.py:237
  130.6 0.1 multiply_reduce_fusion
  130.7 0.3 abs_reduce_fusion.2
  131.0 0.3 convert_convert_fusion.2
  131.5 1.9 %collective-permute-start.14 = (s16[48,2176]{1,0:T(8,128)(2,1)S(1)}, s16[48,2176]{1,0:T(8,128)(2,1)S(1)}, u32[]{:S(2)}, u32[]{:S(2)}) collective-permute-start(s16[48,2176]{1,0:T(8,128)(2,1)S(1)} %get-tuple-element.36), channel_id=1, source_target_pairs={{0,16},{4,20},{8,24},{12,28},{16,0},{20,4},{24,8},{28,12},{1,17},{... | collective-permute-start | bytes 626696 | tf_op jit(solution)/shard_map/ppermute | solution.py:241
  133.5 0.4 collective-permute-done.16
  133.9 0.1 multiply_reduce_fusion.1
  134.0 4.6 %collective-permute-done.15 = s16[48,2176]{1,0:T(8,128)(2,1)S(1)} collective-permute-done((s16[48,2176]{1,0:T(8,128)(2,1)S(1)}, s16[48,2176]{1,0:T(8,128)(2,1)S(1)}, u32[]{:S(2)}, u32[]{:S(2)}) %collective-permute-start.15) | collective-permute-done | bytes 208928 | tf_op jit(solution)/shard_map/ppermute | solution.py:241
  138.7 0.1 multiply_reduce_fusion.3
  138.8 8.5 %collective-permute-done.14 = s16[48,2176]{1,0:T(8,128)(2,1)S(1)} collective-permute-done((s16[48,2176]{1,0:T(8,128)(2,1)S(1)}, s16[48,2176]{1,0:T(8,128)(2,1)S(1)}, u32[]{:S(2)}, u32[]{:S(2)}) %collective-permute-start.14) | collective-permute-done | bytes 208928 | tf_op jit(solution)/shard_map/ppermute | solution.py:241
  147.2 0.1 multiply_reduce_fusion.4
  147.4 1.4 convolution_add_fusion
  (48 shorter events, 0.9 us)
Async XLA Ops:
  0.0 147.4 %copy-start = (f32[16,2048]{1,0:T(8,128)S(1)}, f32[16,2048]{1,0:T(8,128)}, u32[]{:S(2)}) copy-start(f32[16,2048]{1,0:T(8,128)} %param.9) | copy-start | bytes 393220
  1.7 26.2 %collective-permute-start.5 = (bf16[512,8,128]{2,1,0:T(8,128)(2,1)S(1)}, bf16[512,8,128]{2,1,0:T(8,128)(2,1)S(1)}, u32[]{:S(2)}, u32[]{:S(2)}) collective-permute-start(bf16[512,8,128]{2,1,0:T(8,128)(2,1)S(1)} %bitcast.39), channel_id=1, source_target_pairs={{0,2},{1,3},{2,0},{3,1},{4,6},{5,7},{6,4},{7,5},{8,10},{9,11},{10,... | collective-permute-start | bytes 3145736 | tf_op jit(solution)/shard_map/ppermute | solution.py:256
  10.5 12.7 %copy-start.1 = (s32[384]{0:T(512)S(1)}, s32[384]{0:T(512)}, u32[]{:S(2)}) copy-start(s32[384]{0:T(512)} %act_ref.1) | copy-start | bytes 4612
  18.1 10.3 %collective-permute-start.2 = (f32[16,2048]{1,0:T(8,128)}, f32[16,2048]{1,0:T(8,128)}, u32[]{:S(2)}, u32[]{:S(2)}) collective-permute-start(f32[16,2048]{1,0:T(8,128)} %convert_reduce_fusion), channel_id=1, source_target_pairs={{0,24},{4,28},{8,0},{12,4},{16,8},{20,12},{24,16},{28,20},{1,25},{... | collective-permute-start | bytes 393224 | tf_op jit(solution)/shard_map/ppermute | solution.py:241
  21.7 11.7 %collective-permute-start.1 = (f32[16,2048]{1,0:T(8,128)}, f32[16,2048]{1,0:T(8,128)}, u32[]{:S(2)}, u32[]{:S(2)}) collective-permute-start(f32[16,2048]{1,0:T(8,128)} %convert_reduce_fusion), channel_id=1, source_target_pairs={{0,16},{4,20},{8,24},{12,28},{16,0},{20,4},{24,8},{28,12},{1,17},{... | collective-permute-start | bytes 393224 | tf_op jit(solution)/shard_map/ppermute | solution.py:241
  21.7 27.3 %collective-permute-start.6 = (bf16[512,8,128]{2,1,0:T(8,128)(2,1)S(1)}, bf16[512,8,128]{2,1,0:T(8,128)(2,1)S(1)}, u32[]{:S(2)}, u32[]{:S(2)}) collective-permute-start(bf16[512,8,128]{2,1,0:T(8,128)(2,1)S(1)} %bitcast.40), channel_id=1, source_target_pairs={{0,1},{1,0},{2,3},{3,2},{4,5},{5,4},{6,7},{7,6},{8,9},{9,8},{10,11... | collective-permute-start | bytes 3145736 | tf_op jit(solution)/shard_map/ppermute | solution.py:256
  21.7 27.3 %collective-permute-start.4 = (s16[512,1024]{1,0:T(8,128)(2,1)}, s16[512,1024]{1,0:T(8,128)(2,1)}, u32[]{:S(2)}, u32[]{:S(2)}) collective-permute-start(s16[512,1024]{1,0:T(8,128)(2,1)} %fusion.7), channel_id=1, source_target_pairs={{0,4},{4,0},{8,12},{12,8},{16,20},{20,16},{24,28},{28,24},{1,5},{5... | collective-permute-start | bytes 3145736 | tf_op jit(solution)/shard_map/ppermute | solution.py:237
  27.9 21.1 %collective-permute-start.7 = (bf16[512,8,128]{2,1,0:T(8,128)(2,1)S(1)}, bf16[512,8,128]{2,1,0:T(8,128)(2,1)}, u32[]{:S(2)}, u32[]{:S(2)}) collective-permute-start(bf16[512,8,128]{2,1,0:T(8,128)(2,1)S(1)} %collective-permute-done.5.refs_1_), channel_id=1, source_target_pairs={{0,1},{1,0},{2,3},{3,2},{4,5},{5,4},{6,7},{7,6},{8,9},{9,8},{10,11... | collective-permute-start | bytes 3145736 | tf_op jit(solution)/shard_map/ppermute | solution.py:256
  28.4 8.2 %collective-permute-start = (f32[16,2048]{1,0:T(8,128)}, f32[16,2048]{1,0:T(8,128)S(1)}, u32[]{:S(2)}, u32[]{:S(2)}) collective-permute-start(f32[16,2048]{1,0:T(8,128)} %convert_reduce_fusion), channel_id=1, source_target_pairs={{0,8},{4,12},{8,16},{12,20},{16,24},{20,28},{24,0},{28,4},{1,9},{5... | collective-permute-start | bytes 393224 | tf_op jit(solution)/shard_map/ppermute | solution.py:241
  33.4 15.6 %collective-permute-start.3 = (s32[12288]{0:T(1024)S(1)}, s32[12288]{0:T(1024)S(1)}, u32[]{:S(2)}, u32[]{:S(2)}) collective-permute-start(s32[12288]{0:T(1024)S(1)} %add_multiply_fusion.own_idx_ref), channel_id=1, source_target_pairs={{0,4},{4,0},{8,12},{12,8},{16,20},{20,16},{24,28},{28,24},{1,5},{5... | collective-permute-start | bytes 147464 | tf_op jit(solution)/shard_map/ppermute | solution.py:237
  37.7 39.5 %collective-permute-start.11 = (f32[16,2048]{1,0:T(8,128)S(1)}, f32[16,2048]{1,0:T(8,128)S(1)}, u32[]{:S(2)}, u32[]{:S(2)}) collective-permute-start(f32[16,2048]{1,0:T(8,128)S(1)} %add_add_fusion), channel_id=1, source_target_pairs={{0,4},{4,0},{8,12},{12,8},{16,20},{20,16},{24,28},{28,24},{1,5},{5... | collective-permute-start | bytes 393224 | tf_op jit(solution)/shard_map/ppermute | solution.py:237
  73.9 1.9 %copy-start.2 = (f32[384,8,128]{2,1,0:T(8,128)S(1)}, f32[384,8,128]{2,1,0:T(8,128)}, u32[]{:S(2)}) copy-start(f32[384,8,128]{2,1,0:T(8,128)} %get-tuple-element.15) | copy-start | bytes 4718596
  76.4 6.7 %collective-permute-start.10 = (s16[416,256]{1,0:T(8,128)(2,1)S(1)}, s16[416,256]{1,0:T(8,128)(2,1)S(1)}, u32[]{:S(2)}, u32[]{:S(2)}) collective-permute-start(s16[416,256]{1,0:T(8,128)(2,1)S(1)} %get-tuple-element.32), channel_id=1, source_target_pairs={{0,24},{4,28},{8,0},{12,4},{16,8},{20,12},{24,16},{28,20},{1,25},{... | collective-permute-start | bytes 638984 | tf_op jit(solution)/shard_map/ppermute | solution.py:241
  77.6 20.1 %collective-permute-start.9 = (s16[416,256]{1,0:T(8,128)(2,1)S(1)}, s16[416,256]{1,0:T(8,128)(2,1)S(1)}, u32[]{:S(2)}, u32[]{:S(2)}) collective-permute-start(s16[416,256]{1,0:T(8,128)(2,1)S(1)} %get-tuple-element.33), channel_id=1, source_target_pairs={{0,16},{4,20},{8,24},{12,28},{16,0},{20,4},{24,8},{28,12},{1,17},{... | collective-permute-start | bytes 638984 | tf_op jit(solution)/shard_map/ppermute | solution.py:241
  79.8 17.8 %collective-permute-start.8 = (s16[416,256]{1,0:T(8,128)(2,1)S(1)}, s16[416,256]{1,0:T(8,128)(2,1)S(1)}, u32[]{:S(2)}, u32[]{:S(2)}) collective-permute-start(s16[416,256]{1,0:T(8,128)(2,1)S(1)} %get-tuple-element.31), channel_id=1, source_target_pairs={{0,8},{4,12},{8,16},{12,20},{16,24},{20,28},{24,0},{28,4},{1,9},{5... | collective-permute-start | bytes 638984 | tf_op jit(solution)/shard_map/ppermute | solution.py:241
  111.4 14.1 %collective-permute-start.12 = (s16[96,2176]{1,0:T(8,128)(2,1)S(1)}, s16[96,2176]{1,0:T(8,128)(2,1)S(1)}, u32[]{:S(2)}, u32[]{:S(2)}) collective-permute-start(s16[96,2176]{1,0:T(8,128)(2,1)S(1)} %get-tuple-element.35), channel_id=1, source_target_pairs={{0,4},{4,0},{8,12},{12,8},{16,20},{20,16},{24,28},{28,24},{1,5},{5... | collective-permute-start | bytes 1253384 | tf_op jit(solution)/shard_map/ppermute | solution.py:237
  113.2 17.4 %collective-permute-start.13 = (s16[96,2176]{1,0:T(8,128)(2,1)S(1)}, s16[96,2176]{1,0:T(8,128)(2,1)S(1)}, u32[]{:S(2)}, u32[]{:S(2)}) collective-permute-start(s16[96,2176]{1,0:T(8,128)(2,1)S(1)} %get-tuple-element.34), channel_id=1, source_target_pairs={{0,4},{4,0},{8,12},{12,8},{16,20},{20,16},{24,28},{28,24},{1,5},{5... | collective-permute-start | bytes 1253384 | tf_op jit(solution)/shard_map/ppermute | solution.py:237
  126.2 7.8 %collective-permute-start.16 = (s16[48,2176]{1,0:T(8,128)(2,1)S(1)}, s16[48,2176]{1,0:T(8,128)(2,1)S(1)}, u32[]{:S(2)}, u32[]{:S(2)}) collective-permute-start(s16[48,2176]{1,0:T(8,128)(2,1)S(1)} %pad_add_fusion.3), channel_id=1, source_target_pairs={{0,8},{4,12},{8,16},{12,20},{16,24},{20,28},{24,0},{28,4},{1,9},{5... | collective-permute-start | bytes 626696 | tf_op jit(solution)/shard_map/ppermute | solution.py:241
  131.4 7.2 %collective-permute-start.15 = (s16[48,2176]{1,0:T(8,128)(2,1)S(1)}, s16[48,2176]{1,0:T(8,128)(2,1)S(1)}, u32[]{:S(2)}, u32[]{:S(2)}) collective-permute-start(s16[48,2176]{1,0:T(8,128)(2,1)S(1)} %get-tuple-element.37), channel_id=1, source_target_pairs={{0,24},{4,28},{8,0},{12,4},{16,8},{20,12},{24,16},{28,20},{1,25},{... | collective-permute-start | bytes 626696 | tf_op jit(solution)/shard_map/ppermute | solution.py:241
  131.5 15.7 %collective-permute-start.14 = (s16[48,2176]{1,0:T(8,128)(2,1)S(1)}, s16[48,2176]{1,0:T(8,128)(2,1)S(1)}, u32[]{:S(2)}, u32[]{:S(2)}) collective-permute-start(s16[48,2176]{1,0:T(8,128)(2,1)S(1)} %get-tuple-element.36), channel_id=1, source_target_pairs={{0,16},{4,20},{8,24},{12,28},{16,0},{20,4},{24,8},{28,12},{1,17},{... | collective-permute-start | bytes 626696 | tf_op jit(solution)/shard_map/ppermute | solution.py:241
